TPU v7x, 32 devices: a whole 2x2x4 slice. The times are simulated.
32 devices in a mesh: row: 2 (over y), col: 4 (over z), depth: 4 (over x, core).
Axes of the slice: x: 2, y: 2, z: 4, core: 2. Of those that a mesh axis runs over, the one named last changes fastest.
Arguments:
- grad_out: bfloat16 [1024, 6144], P('depth', 'col'), may hold values from -6 to 6
- pre_act: bfloat16 [1024, 24576], P('depth', 'row'), may hold values from -8 to 8
- down_weight: bfloat16 [24576, 6144], P(('row', 'depth'), 'col'), may hold values from -0.0546875 to 0.0546875
Outputs:
- grad_pre: bfloat16 [1024, 24576], P('depth', 'row')
- grad_weight: bfloat16 [24576, 6144], P(('row', 'depth'), 'col')
All inputs are finite; a program needn't handle non-finite values.
Results may differ from a plain program's by a relative error of at most 0.0066.
Values may be sent and summed in bfloat16 or wider, within the bound.
A program may use at most 128 MiB of HBM per device.

v0:
```python
import jax
import jax.numpy as jnp
from jax import lax
from jax.sharding import PartitionSpec as P

sqrt_two_pi = 0.7978845608028654
cubic_coeff = 0.044715


def gelu_value(preact):
    tangent = jnp.tanh(sqrt_two_pi * (preact + cubic_coeff * preact * preact * preact))
    return 0.5 * preact * (1.0 + tangent)


def gelu_slope(preact):
    tangent = jnp.tanh(sqrt_two_pi * (preact + cubic_coeff * preact * preact * preact))
    inner = sqrt_two_pi * (1.0 + 3.0 * cubic_coeff * preact * preact)
    return 0.5 * (1.0 + tangent) + 0.5 * preact * (1.0 - tangent * tangent) * inner


def contract_last(left, right):
    return lax.dot_general(
        left, right, (((1,), (1,)), ((), ())), preferred_element_type=jnp.float32
    )


def contract_first(left, right):
    return lax.dot_general(
        left, right, (((0,), (0,)), ((), ())), preferred_element_type=jnp.float32
    )


def finish_rows(partial_value, preacts):
    total = lax.psum(partial_value, "col")
    return (total * gelu_slope(preacts.astype(jnp.float32))).astype(jnp.bfloat16)


def on_device(grad_out, pre_act, down_weight):
    every_grad = lax.all_gather(grad_out, "depth", axis=0, tiled=True)
    own_pre = lax.all_to_all(pre_act, "depth", split_axis=1, concat_axis=0, tiled=True)
    partial_value = contract_last(every_grad, down_weight)
    local_grad = finish_rows(partial_value, own_pre)
    grad_pre = lax.all_to_all(local_grad, "depth", split_axis=0, concat_axis=1, tiled=True)
    own_act = gelu_value(own_pre.astype(jnp.float32)).astype(jnp.bfloat16)
    grad_weight = contract_first(own_act, every_grad).astype(jnp.bfloat16)
    return (grad_pre, grad_weight)


def solution(mesh):
    placed = (P("depth", "col"), P("depth", "row"), P(("row", "depth"), "col"))
    return jax.shard_map(
        on_device,
        mesh=mesh,
        in_specs=placed,
        out_specs=(P("depth", "row"), P(("row", "depth"), "col")),
        check_vma=False,
    )
```

profile of v0, /device:TPU:0, one launch (start us, length us, event | category | flops | bytes accessed | tf_op | source)
XLA Modules:
  0.0 588.5 jit_solution(14912220487641829081)
XLA Ops:
  7.2 0.0 all-gather.2.cloned.1.call-start
  7.2 0.7 all-gather.2.cloned.1.call-update
  7.9 0.0 all-reduce.2.cloned.1.call-start
  7.9 32.8 %all-gather.2.cloned.1.call-done = bf16[1024,1536]{1,0:T(8,128)(2,1)} async-done(((bf16[256,1536]{1,0:T(8,128)(2,1)}), bf16[1024,1536]{1,0:T(8,128)(2,1)}) %all-gather.2.cloned.1.call-update) | async-done | bytes 3145744 | tf_op jit(solution)/shard_map/all_gather | solution.py:39
  40.8 16.2 %fusion.11 = f32[1024,3072]{1,0:T(8,128)} fusion(bf16[1024,1536]{1,0:T(8,128)(2,1)} %all-gather.2.cloned.1.call-done, bf16[3072,1536]{1,0:T(8,128)(2,1)} %param.5), kind=kOutput, calls=%fused_computation.16 | convolution fusion | flops 9663676416 | bytes 25165824 | tf_op jit(solution)/shard_map/dot_general | solution.py:22
  57.0 0.0 all-reduce.2.cloned.1.call-update
  57.0 3.2 copy.10
  60.2 74.3 %all_to_all.32 = bf16[256,4,3072]{2,0,1:T(8,128)(2,1)} all-to-all(bf16[256,4,3072]{2,0,1:T(8,128)(2,1)S(1)} %bitcast.30), channel_id=1, replica_groups=mesh['row'=2,'col'=4,'depth'=4] {'depth'}, dimensions={1} | all-to-all | bytes 12582912 | tf_op jit(solution)/shard_map/all_to_all | solution.py:40
  134.5 348.8 %all-reduce.2.cloned.1.call-done = f32[1024,3072]{1,0:T(8,128)} async-done(((f32[1024,3072]{1,0:T(8,128)}), f32[1024,3072]{1,0:T(8,128)}) %all-reduce.2.cloned.1.call-update) | async-done | bytes 12582928 | tf_op jit(solution)/shard_map/psum | solution.py:34
  483.3 16.1 %fusion.10 = (bf16[1024,3072]{1,0:T(8,128)(2,1)}, bf16[1024,3072]{1,0:T(8,128)(2,1)}) fusion(bf16[256,4,3072]{2,0,1:T(8,128)(2,1)} %all_to_all.32, f32[1024,3072]{1,0:T(8,128)} %all-reduce.2.cloned.1.call-done), kind=kLoop, calls=%fused_computation.13 | loop fusion | flops 69206016 | bytes 31457280 | tf_op jit(solution)/shard_map/convert_element_type | solution.py:44
  499.4 0.0 copy-start
  499.4 5.5 all-to-all-start.1
  504.9 0.0 copy-done
  504.9 14.9 %convolution_convert_fusion = bf16[3072,1536]{1,0:T(8,128)(2,1)} fusion(bf16[1024,3072]{1,0:T(8,128)(2,1)} %get-tuple-element.2, bf16[1024,1536]{1,0:T(8,128)(2,1)S(1)} %copy-done), kind=kOutput, calls=%fused_computation.14 | convolution fusion | flops 9668395008 | bytes 18874368 | tf_op jit(solution)/shard_map/dot_general | solution.py:28
  519.8 55.7 %all-to-all-done.1 = bf16[4,256,3072]{2,1,0:T(8,128)(2,1)} async-done(((bf16[4,256,3072]{2,1,0:T(8,128)(2,1)}), bf16[4,256,3072]{2,1,0:T(8,128)(2,1)}, u32[]{:S(2)}, u32[]{:S(2)}) %all-to-all-start.1) | async-done | bytes 6291488 | tf_op jit(solution)/shard_map/all_to_all | solution.py:43
  575.6 6.1 %copy.8 = bf16[4,32,8,3072]{3,2,0,1:T(8,128)(2,1)} copy(bf16[4,32,8,3072]{3,2,1,0:T(8,128)(2,1)} %bitcast.7) | data formatting | bytes 12582912 | tf_op jit(solution)/shard_map/all_to_all | solution.py:43
Async XLA Ops:
  7.2 33.6 %all-gather.2.cloned.1.call-start = ((), (), s32[]{:S(2)}) async-start(), calls=%async_computation.2 | async-start | bytes 3932160 | tf_op jit(solution)/shard_map/all_gather | solution.py:39
  7.9 475.4 %all-reduce.2.cloned.1.call-start = ((), (), s32[]{:S(2)}) async-start(), calls=%async_computation.3 | async-start | bytes 25165824 | tf_op jit(solution)/shard_map/psum | solution.py:34
  499.4 5.5 copy-start
  499.4 76.2 %all-to-all-start.1 = ((bf16[4,256,3072]{2,1,0:T(8,128)(2,1)}), bf16[4,256,3072]{2,1,0:T(8,128)(2,1)}, u32[]{:S(2)}, u32[]{:S(2)}) async-start(bf16[4,256,3072]{2,1,0:T(8,128)(2,1)} %bitcast.31), calls=%async_computation.1 | async-start | bytes 12582912 | tf_op jit(solution)/shard_map/all_to_all | solution.py:43
Sparse Core Ops, SparseCore 0:
  9.5 31.2 all-gather.1
  57.1 426.1 all-reduce.1
where the time goes:
time: 589 us
  waiting for transfers between devices  438 us (74%)
  blocking collectives  74.3 us (13%)
  matrix products  31.1 us (5%)
  other arithmetic  16.1 us (3%)
  between operations  14.1 us (2%)
  local copies, waits for them, and re-layouts  9.36 us (2%)
    psum x1, waiting for transfers between devices, finish_rows(): total = lax.psum(partial_value, 'col')  349 us
    all_to_all x1, blocking collectives, on_device(): lax.all_to_all(pre_act, 'depth', split_axis=1, concat_axis=0, tiled=True)  74.3 us
    all_to_all x1, waiting for transfers between devices, on_device(): lax.all_to_all(local_grad, 'depth', split_axis=0, concat_axis=1, tiled=True)  55.7 us
    all_gather x1, waiting for transfers between devices, on_device(): every_grad = lax.all_gather(grad_out, 'depth', axis=0, tiled=True)  32.8 us
    dot_general x1, matrix products, contract_last(): lax.dot_general(left, right, (((1,), (1,)), ((), ())), preferred_element_...  16.2 us
    convert_element_type x1, other arithmetic, on_device(): own_act = gelu_value(own_pre.astype(jnp.float32)).astype(jnp.bfloat16)  16.1 us
    dot_general x1, matrix products, contract_first(): lax.dot_general(left, right, (((0,), (0,)), ((), ())), preferred_element_...  14.9 us
  transfers between devices with their start and end apart: 3, of which 3 were waited for; matrix products, arithmetic and copies ran while one was open for 3% of the time, Pallas kernels for 0%

commit v1 on v0

--- a/solution.py
+++ b/solution.py
@@ -31,7 +31,9 @@
 
 
 def finish_rows(partial_value, preacts):
-    total = lax.psum(partial_value, "col")
+    total = partial_value
+    for hop in (1, 2):
+        total = total + lax.ppermute(total, "col", [(dev, dev ^ hop) for dev in range(4)])
     return (total * gelu_slope(preacts.astype(jnp.float32))).astype(jnp.bfloat16)
 
 

time: 589 us -> 984 us (1.67)
  waiting for transfers between devices: 438 us -> 820 us
    ppermute x0 -> x2, waiting for transfers between devices: none -> 731 us  [finish_rows(): lax.ppermute(total, 'col', [(dev, dev ^ hop) for dev in range(4)])]
    psum x1 -> x0, waiting for transfers between devices: 349 us -> none  [finish_rows(): total = lax.psum(partial_value, 'col')]
  transfers between devices with their start and end apart: 3 -> 4, of which waited for: 3 -> 4; matrix products, arithmetic and copies ran while one was open for 3% -> 2% of each run, Pallas kernels for 0% -> 0%
where the time goes in v1:
time: 984 us
  waiting for transfers between devices  820 us (83%)
  blocking collectives  74.2 us (8%)
  matrix products  28.4 us (3%)
  other arithmetic  25.5 us (3%)
  between operations  14.1 us (1%)
  local copies, waits for them, and re-layouts  12.3 us (1%)
    ppermute x2, waiting for transfers between devices, finish_rows(): lax.ppermute(total, 'col', [(dev, dev ^ hop) for dev in range(4)])  731 us
    all_to_all x1, blocking collectives, on_device(): lax.all_to_all(pre_act, 'depth', split_axis=1, concat_axis=0, tiled=True)  74.2 us
    all_to_all x1, waiting for transfers between devices, on_device(): lax.all_to_all(local_grad, 'depth', split_axis=0, concat_axis=1, tiled=True)  55.6 us
    all_gather x1, waiting for transfers between devices, on_device(): every_grad = lax.all_gather(grad_out, 'depth', axis=0, tiled=True)  32.9 us
  transfers between devices with their start and end apart: 4, of which 4 were waited for; matrix products, arithmetic and copies ran while one was open for 2% of the time, Pallas kernels for 0%

profile of v1, /device:TPU:0, one launch (start us, length us, event | category | flops | bytes accessed | tf_op | source)
XLA Modules:
  0.0 983.9 jit_solution(17481418890469063984)
XLA Ops:
  7.2 0.0 all-gather.2.cloned.1.call-start
  7.2 0.7 all-gather.2.cloned.1.call-update
  7.9 32.9 %all-gather.2.cloned.1.call-done = bf16[1024,1536]{1,0:T(8,128)(2,1)} async-done(((bf16[256,1536]{1,0:T(8,128)(2,1)}), bf16[1024,1536]{1,0:T(8,128)(2,1)}) %all-gather.2.cloned.1.call-update) | async-done | bytes 3145744 | tf_op jit(solution)/shard_map/all_gather | solution.py:41
  40.8 13.5 %fusion.11 = f32[1024,3072]{1,0:T(8,128)S(1)} fusion(bf16[1024,1536]{1,0:T(8,128)(2,1)} %all-gather.2.cloned.1.call-done, bf16[3072,1536]{1,0:T(8,128)(2,1)} %param.5), kind=kOutput, calls=%fused_computation.16 | convolution fusion | flops 9663676416 | bytes 25165824 | tf_op jit(solution)/shard_map/dot_general | solution.py:22
  54.3 0.0 copy-start
  54.3 1.6 collective-permute-start
  55.8 3.0 copy-done
  58.8 268.1 %collective-permute-done = f32[1024,3072]{1,0:T(8,128)} collective-permute-done((f32[1024,3072]{1,0:T(8,128)S(1)}, f32[1024,3072]{1,0:T(8,128)}, u32[]{:S(2)}, u32[]{:S(2)}) %collective-permute-start) | collective-permute-done | bytes 12582944 | tf_op jit(solution)/shard_map/ppermute | solution.py:36
  326.9 9.5 add.20
  336.4 2.5 collective-permute-start.1
  338.9 3.2 copy.10
  342.1 74.2 %all_to_all.32 = bf16[256,4,3072]{2,0,1:T(8,128)(2,1)} all-to-all(bf16[256,4,3072]{2,0,1:T(8,128)(2,1)S(1)} %bitcast.30), channel_id=1, replica_groups=mesh['row'=2,'col'=4,'depth'=4] {'depth'}, dimensions={1} | all-to-all | bytes 12582912 | tf_op jit(solution)/shard_map/all_to_all | solution.py:42
  416.3 462.4 %collective-permute-done.1 = f32[1024,3072]{1,0:T(8,128)} collective-permute-done((f32[1024,3072]{1,0:T(8,128)S(1)}, f32[1024,3072]{1,0:T(8,128)}, u32[]{:S(2)}, u32[]{:S(2)}) %collective-permute-start.1) | collective-permute-done | bytes 12582944 | tf_op jit(solution)/shard_map/ppermute | solution.py:36
  878.7 16.1 %fusion.10 = (bf16[1024,3072]{1,0:T(8,128)(2,1)}, bf16[1024,3072]{1,0:T(8,128)(2,1)}) fusion(bf16[256,4,3072]{2,0,1:T(8,128)(2,1)} %all_to_all.32, f32[1024,3072]{1,0:T(8,128)S(1)} %add.20, f32[1024,3072]{1,0:T(8,128)} %collective-permute-done.1), kind=kLoop, calls=%fused_computation.13 | loop fusion | flops 72351744 | bytes 44040192 | tf_op jit(solution)/shard_map/convert_element_type | solution.py:46
  894.8 0.0 copy-start.1
  894.8 5.7 all-to-all-start.1
  900.5 0.0 copy-done.1
  900.5 14.9 %convolution_convert_fusion = bf16[3072,1536]{1,0:T(8,128)(2,1)} fusion(bf16[1024,3072]{1,0:T(8,128)(2,1)} %get-tuple-element.2, bf16[1024,1536]{1,0:T(8,128)(2,1)S(1)} %copy-done.1), kind=kOutput, calls=%fused_computation.14 | convolution fusion | flops 9668395008 | bytes 18874368 | tf_op jit(solution)/shard_map/dot_general | solution.py:28
  915.4 55.6 %all-to-all-done.1 = bf16[4,256,3072]{2,1,0:T(8,128)(2,1)} async-done(((bf16[4,256,3072]{2,1,0:T(8,128)(2,1)}), bf16[4,256,3072]{2,1,0:T(8,128)(2,1)}, u32[]{:S(2)}, u32[]{:S(2)}) %all-to-all-start.1) | async-done | bytes 6291488 | tf_op jit(solution)/shard_map/all_to_all | solution.py:45
  971.0 6.1 copy.8
Async XLA Ops:
  7.2 33.6 %all-gather.2.cloned.1.call-start = ((), (), s32[]{:S(2)}) async-start(), calls=%async_computation.2 | async-start | bytes 3932160 | tf_op jit(solution)/shard_map/all_gather | solution.py:41
  54.3 4.5 copy-start
  54.3 272.6 %collective-permute-start = (f32[1024,3072]{1,0:T(8,128)S(1)}, f32[1024,3072]{1,0:T(8,128)}, u32[]{:S(2)}, u32[]{:S(2)}) collective-permute-start(f32[1024,3072]{1,0:T(8,128)S(1)} %fusion.11), channel_id=1, source_target_pairs={{0,4},{4,0},{8,12},{12,8},{1,5},{5,1},{9,13},{13,9},{2,6},{6,2},{1... | collective-permute-start | bytes 37748744 | tf_op jit(solution)/shard_map/ppermute | solution.py:36
  336.4 542.3 %collective-permute-start.1 = (f32[1024,3072]{1,0:T(8,128)S(1)}, f32[1024,3072]{1,0:T(8,128)}, u32[]{:S(2)}, u32[]{:S(2)}) collective-permute-start(f32[1024,3072]{1,0:T(8,128)S(1)} %add.20), channel_id=1, source_target_pairs={{0,8},{4,12},{8,0},{12,4},{1,9},{5,13},{9,1},{13,5},{2,10},{6,14},... | collective-permute-start | bytes 37748744 | tf_op jit(solution)/shard_map/ppermute | solution.py:36
  894.8 5.7 copy-start.1
  894.8 76.2 %all-to-all-start.1 = ((bf16[4,256,3072]{2,1,0:T(8,128)(2,1)}), bf16[4,256,3072]{2,1,0:T(8,128)(2,1)}, u32[]{:S(2)}, u32[]{:S(2)}) async-start(bf16[4,256,3072]{2,1,0:T(8,128)(2,1)} %bitcast.31), calls=%async_computation.1 | async-start | bytes 12582912 | tf_op jit(solution)/shard_map/all_to_all | solution.py:45
Sparse Core Ops, SparseCore 0:
  9.5 31.2 all-gather.1
